TPU v7x, 32 devices: a 4x4x1 block of a 4x4x8 slice. The times are simulated.
32 devices in a mesh: rep: 1 (over z), dp: 32 (over x, y, core).
Axes of the slice: x: 4, y: 4, z: 1, core: 2. Of those that a mesh axis runs over, the one named last changes fastest.
The devices are a block of a 4x4x8 slice.
Arguments:
- g_w_gate: bfloat16 [32, 2, 1024, 3328], P(('rep', 'dp'))
- g_w_up: bfloat16 [32, 2, 1024, 3328], P(('rep', 'dp'))
- g_w_down: bfloat16 [32, 2, 3328, 1024], P(('rep', 'dp'))
- w_gate: bfloat16 [2, 1024, 3328], replicated
- w_up: bfloat16 [2, 1024, 3328], replicated
- w_down: bfloat16 [2, 3328, 1024], replicated
- m_w_gate: float32 [2, 1024, 3328], P(None, 'dp')
- m_w_up: float32 [2, 1024, 3328], P(None, 'dp')
- m_w_down: float32 [2, 3328, 1024], P(None, 'dp')
- v_w_gate: float32 [2, 1024, 3328], P(None, 'dp')
- v_w_up: float32 [2, 1024, 3328], P(None, 'dp')
- v_w_down: float32 [2, 3328, 1024], P(None, 'dp')
Outputs:
- output 1: bfloat16 [2, 1024, 3328], P('rep')
- output 2: bfloat16 [2, 1024, 3328], P('rep')
- output 3: bfloat16 [2, 3328, 1024], P('rep')
- output 4: float32 [2, 1024, 3328], P('rep', 'dp')
- output 5: float32 [2, 1024, 3328], P('rep', 'dp')
- output 6: float32 [2, 3328, 1024], P('rep', 'dp')
- output 7: float32 [2, 1024, 3328], P('rep', 'dp')
- output 8: float32 [2, 1024, 3328], P('rep', 'dp')
- output 9: float32 [2, 3328, 1024], P('rep', 'dp')
All inputs are finite; a program needn't handle non-finite values.
Results may differ from a plain program's by a relative error of at most 0.022.
Values are sent between devices in bfloat16 or wider.
A program may use at most 768 MiB of HBM per device.

v0:
```python
import jax
import jax.numpy as jnp
from jax import lax
from jax.sharding import PartitionSpec as P


def adamw(w, m, v, g):
    m = 0.9 * m + 0.1 * g
    v = 0.95 * v + 0.05 * g * g
    step = m * lax.rsqrt(v + 1e-8) + 0.1 * w
    return (w - 0.02 * step).astype(jnp.bfloat16), m, v


def solution(mesh):
    def step(*arrays):
        terms, weights, m, v = (arrays[i : i + 3] for i in (0, 3, 6, 9))
        gradients = [lax.psum_scatter(t[0], "dp", scatter_dimension=1, tiled=True).astype(jnp.float32) for t in terms]
        me = lax.axis_index("dp")
        own = [lax.dynamic_slice_in_dim(w, me * one.shape[1], one.shape[1], 1).astype(jnp.float32) for w, one in zip(weights, m, strict=True)]
        new = [adamw(w, m, v, g) for w, m, v, g in zip(own, m, v, gradients, strict=True)]
        whole = [lax.all_gather(one[0], "dp", axis=1, tiled=True) for one in new]
        return (*whole, *(one[1] for one in new), *(one[2] for one in new))

    all_of, cut = P(None, None, None), P(None, "dp", None)
    return jax.shard_map(
        step,
        mesh=mesh,
        in_specs=(P(("rep", "dp"), None, None, None),) * 3 + (all_of,) * 3 + (cut,) * 6,
        out_specs=(P("rep", None, None),) * 3 + (P("rep", "dp", None),) * 6,
        check_vma=False,
    )
```

profile of v0, /device:TPU:97, one launch (start us, length us, event | category | flops | bytes accessed | tf_op | source)
XLA Modules:
  0.0 540.4 jit_solution(5334104977659056398)
XLA Ops:
  7.2 0.1 reduce-scatter.8.cloned.1.call-start
  7.3 0.7 reduce-scatter.8.cloned.1.call-update
  8.0 0.1 reduce-scatter.6.cloned.1.call-start
  8.1 0.7 reduce-scatter.6.cloned.1.call-update
  8.8 0.1 reduce-scatter.10.cloned.1.call-start
  8.9 22.9 %copy.21 = bf16[2,3328,1024]{2,0,1:T(2,128)(2,1)S(1)} copy(bf16[2,3328,1024]{2,1,0:T(8,128)(2,1)} %bitcast.9) | data formatting | bytes 27262976
  31.8 7.8 %copy.23 = bf16[416,8,2,1024]{3,1,2,0:T(8,128)(2,1)} copy(bf16[416,8,2,1024]{3,2,1,0:T(2,128)(2,1)S(1)} %bitcast.8) | data formatting | bytes 27262976
  39.6 0.0 copy-start.1
  39.6 0.0 copy-start.2
  39.6 0.0 copy-start.3
  39.6 0.0 copy-start.4
  39.6 0.1 reduce-scatter.10.cloned.1.call-update
  39.7 0.1 all-gather.6.cloned.1.call-start
  39.8 73.1 %reduce-scatter.8.cloned.1.call-done = bf16[2,32,3328]{2,1,0:T(8,128)(2,1)} async-done(((bf16[2,1024,3328]{2,1,0:T(8,128)(2,1)}), bf16[2,32,3328]{2,1,0:T(8,128)(2,1)}) %reduce-scatter.8.cloned.1.call-update) | async-done | bytes 426000 | tf_op jit(solution)/shard_map/reduce_scatter | solution.py:17
  112.9 0.0 copy-done.1
  112.9 0.0 copy-done.2
  112.9 2.6 fusion.6
  115.6 0.1 all-gather.6.cloned.1.call-update
  115.6 0.1 all-gather.4.cloned.1.call-start
  115.7 99.6 %reduce-scatter.6.cloned.1.call-done = bf16[2,32,3328]{2,1,0:T(8,128)(2,1)} async-done(((bf16[2,1024,3328]{2,1,0:T(8,128)(2,1)}), bf16[2,32,3328]{2,1,0:T(8,128)(2,1)}) %reduce-scatter.6.cloned.1.call-update) | async-done | bytes 426000 | tf_op jit(solution)/shard_map/reduce_scatter | solution.py:17
  215.3 0.0 copy-done.3
  215.3 0.0 copy-done.4
  215.3 2.6 fusion.2
  217.9 0.1 all-gather.4.cloned.1.call-update
  218.0 0.1 all-gather.8.cloned.1.call-start
  218.1 100.1 %reduce-scatter.10.cloned.1.call-done = bf16[104,2048]{1,0:T(8,128)(2,1)} async-done(((bf16[3328,2048]{1,0:T(8,128)(2,1)}), bf16[104,2048]{1,0:T(8,128)(2,1)}) %reduce-scatter.10.cloned.1.call-update) | async-done | bytes 426000
  318.2 1.3 reshape.19
  319.5 3.2 fusion.10
  322.7 0.1 all-gather.8.cloned.1.call-update
  322.8 59.7 %all-gather.6.cloned.1.call-done = bf16[2,1024,3328]{2,1,0:T(8,128)(2,1)} async-done(((bf16[2,32,3328]{2,1,0:T(8,128)(2,1)}), bf16[2,1024,3328]{2,1,0:T(8,128)(2,1)}) %all-gather.6.cloned.1.call-update) | async-done | bytes 13631504 | tf_op jit(solution)/shard_map/all_gather | solution.py:21
  382.4 61.9 %all-gather.4.cloned.1.call-done = bf16[2,1024,3328]{2,1,0:T(8,128)(2,1)} async-done(((bf16[2,32,3328]{2,1,0:T(8,128)(2,1)}), bf16[2,1024,3328]{2,1,0:T(8,128)(2,1)}) %all-gather.4.cloned.1.call-update) | async-done | bytes 13631504 | tf_op jit(solution)/shard_map/all_gather | solution.py:21
  444.4 61.9 %all-gather.8.cloned.1.call-done = bf16[2,3328,1024]{2,1,0:T(8,128)(2,1)} async-done(((bf16[2,104,1024]{2,1,0:T(8,128)(2,1)}), bf16[2,3328,1024]{2,1,0:T(8,128)(2,1)}) %all-gather.8.cloned.1.call-update) | async-done | bytes 13631504 | tf_op jit(solution)/shard_map/all_gather | solution.py:21
  506.3 0.0 copy-start
  506.3 0.0 slice-start
  506.3 0.0 slice-start.1
  506.3 0.0 slice-start.2
  506.3 15.1 %copy.31 = bf16[2,1024,3328]{2,1,0:T(8,128)(2,1)} copy(bf16[2,1024,3328]{2,1,0:T(8,128)(2,1)} %all-gather.4.cloned.1.call-done) | data formatting | bytes 27262976
  521.4 0.0 copy-done
  521.4 0.0 slice-start.3
  521.4 6.6 %copy.32 = bf16[2,1024,3328]{2,1,0:T(8,128)(2,1)} copy(bf16[2,1024,3328]{2,1,0:T(8,128)(2,1)S(1)} %copy-done) | data formatting | bytes 27262976
  527.9 0.0 slice-done
  527.9 0.0 slice-done.1
  527.9 0.0 slice-done.2
  527.9 0.5 slice-done.3
  528.5 5.1 copy.33
  (1 shorter events, 0.0 us)
Async XLA Ops:
  7.2 105.7 %reduce-scatter.8.cloned.1.call-start = ((), (), s32[]{:S(2)}) async-start(), calls=%async_computation.5 | async-start | bytes 14057472 | tf_op jit(solution)/shard_map/reduce_scatter | solution.py:17
  8.0 207.3 %reduce-scatter.6.cloned.1.call-start = ((), (), s32[]{:S(2)}) async-start(), calls=%async_computation.3 | async-start | bytes 14057472 | tf_op jit(solution)/shard_map/reduce_scatter | solution.py:17
  8.8 309.4 %reduce-scatter.10.cloned.1.call-start = ((), (), s32[]{:S(2)}) async-start(), calls=%async_computation.8 | async-start | bytes 14057472
  39.6 73.3 %copy-start.1 = (f32[2,32,3328]{2,1,0:T(8,128)S(1)}, f32[2,32,3328]{2,1,0:T(8,128)}, u32[]{:S(2)}) copy-start(f32[2,32,3328]{2,1,0:T(8,128)} %param.22) | copy-start | bytes 2555908
  39.6 73.3 %copy-start.2 = (f32[2,32,3328]{2,1,0:T(8,128)S(1)}, f32[2,32,3328]{2,1,0:T(8,128)}, u32[]{:S(2)}) copy-start(f32[2,32,3328]{2,1,0:T(8,128)} %param.19) | copy-start | bytes 2555908
  39.6 175.6 %copy-start.3 = (f32[2,32,3328]{2,1,0:T(8,128)S(1)}, f32[2,32,3328]{2,1,0:T(8,128)}, u32[]{:S(2)}) copy-start(f32[2,32,3328]{2,1,0:T(8,128)} %param.21) | copy-start | bytes 2555908
  39.6 175.6 %copy-start.4 = (f32[2,32,3328]{2,1,0:T(8,128)S(1)}, f32[2,32,3328]{2,1,0:T(8,128)}, u32[]{:S(2)}) copy-start(f32[2,32,3328]{2,1,0:T(8,128)} %param.18) | copy-start | bytes 2555908
  39.7 342.7 %all-gather.6.cloned.1.call-start = ((), (), s32[]{:S(2)}) async-start(), calls=%async_computation.6 | async-start | bytes 14057472 | tf_op jit(solution)/shard_map/all_gather | solution.py:21
  115.6 328.7 %all-gather.4.cloned.1.call-start = ((), (), s32[]{:S(2)}) async-start(), calls=%async_computation.4 | async-start | bytes 14057472 | tf_op jit(solution)/shard_map/all_gather | solution.py:21
  218.0 288.3 %all-gather.8.cloned.1.call-start = ((), (), s32[]{:S(2)}) async-start(), calls=%async_computation.7 | async-start | bytes 14057472 | tf_op jit(solution)/shard_map/all_gather | solution.py:21
  506.3 15.1 %copy-start = (bf16[2,1024,3328]{2,1,0:T(8,128)(2,1)S(1)}, bf16[2,1024,3328]{2,1,0:T(8,128)(2,1)}, u32[]{:S(2)}) copy-start(bf16[2,1024,3328]{2,1,0:T(8,128)(2,1)} %all-gather.6.cloned.1.call-done) | copy-start | bytes 40894468
  506.3 21.6 %slice-start = ((s8[13631488]{0:T(1024)(128)(4,1)}), s8[4194304]{0:T(1024)(128)(4,1)S(1)}, s32[]{:S(2)}) async-start(s8[13631488]{0:T(1024)(128)(4,1)} %bitcast.12), calls=%async_computation.9 | async-start | bytes 8388608
  506.3 21.6 %slice-start.1 = ((s8[13631488]{0:T(1024)(128)(4,1)}), s8[4194304]{0:T(1024)(128)(4,1)S(1)}, s32[]{:S(2)}) async-start(s8[13631488]{0:T(1024)(128)(4,1)} %bitcast.12), calls=%async_computation.10 | async-start | bytes 8388608
  506.3 21.6 %slice-start.2 = ((s8[13631488]{0:T(1024)(128)(4,1)}), s8[4194304]{0:T(1024)(128)(4,1)S(1)}, s32[]{:S(2)}) async-start(s8[13631488]{0:T(1024)(128)(4,1)} %bitcast.12), calls=%async_computation.11 | async-start | bytes 8388608
  521.4 7.1 %slice-start.3 = ((s8[13631488]{0:T(1024)(128)(4,1)}), s8[1048576]{0:T(1024)(128)(4,1)S(1)}, s32[]{:S(2)}) async-start(s8[13631488]{0:T(1024)(128)(4,1)} %bitcast.12), calls=%async_computation.12 | async-start | bytes 2097152
Sparse Core Ops, SparseCore 0:
  11.7 101.1 reduce-scatter.7
  116.6 98.6 reduce-scatter.5
  219.5 98.6 reduce-scatter.9
  320.8 61.6 all-gather.5
  385.0 59.3 all-gather.3
  446.9 59.3 all-gather.7
where the time goes:
time: 541 us; the launch traced here: 540 us
  waiting for transfers between devices  458 us (85%)
  local copies, waits for them, and re-layouts  59.4 us (11%)
  between operations  14.2 us (3%)
  other arithmetic  8.47 us (2%)
    all_gather x3, waiting for transfers between devices, step(): whole = [lax.all_gather(one[0], 'dp', axis=1, tiled=True) for one in new]  184 us
    reduce_scatter x2, waiting for transfers between devices, step(): lax.psum_scatter(t[0], 'dp', scatter_dimension=1, tiled=True)  173 us
    unnamed x7, waiting for transfers between devices  102 us
    unnamed x24, local copies, waits for them, and re-layouts  59.4 us
  transfers between devices with their start and end apart: 6, of which 6 were waited for; matrix products, arithmetic and copies ran while one was open for 8% of the time, Pallas kernels for 0%

commit v1 on v0

v1 whole, which is shorter than its diff:
```python
import functools
import math

import jax
import jax.numpy as jnp
from jax import lax
from jax.experimental import pallas as pl
from jax.experimental.pallas import tpu as pltpu
from jax.sharding import PartitionSpec as P

F32, BF16 = jnp.float32, jnp.bfloat16
RING = 4
CORES = 2
PER_MATRIX = 2
VMEM_LIMIT = 17050 << 10
EARLY_SLOTS = 2
SLOTS = 3

TURN = {'send_half': (-17.7, 10.6), 'load_half': (-8.4, 10.6), 'load_other': (-8.0, 10.6), 'rs1': (-3.6, 10.6), 'rs1_relay_load': (3.5, 10.6), 'rs1_relay': (5.0, 10.6), 'rs2_load': (12.4, 10.6), 'rs2': (13.3, 10.6), 'rs2_relay': (17.1, 10.6), 'update': (21.6, 10.6), 'ag1_own': (24.0, 12.24), 'ag2_relay': (24.8, 12.24), 'ag1_near': (25.3, 12.24), 'ag1_far': (31.0, 12.24), 'ag1_relay': (44.8, 12.24), 'ag1_relay_far': (48.3, 12.24), 'last': (66.1, 12.24)}


def as_tiles(a, rows):
    *lead, r, c = a.shape
    n = len(lead)
    a = a.reshape(*lead, r // 8, 8, c // 128, 128).transpose(*range(n), n, n + 2, n + 1, n + 3)
    return a.reshape(*lead, r // rows, rows // 8 * (c // 128), 8, 128)


def from_tiles(a, rows, columns):
    lead = a.shape[: a.ndim - 4]
    n = len(lead)
    a = a.reshape(*lead, rows // 8, columns // 128, 8, 128).transpose(*range(n), n, n + 2, n + 1, n + 3)
    return a.reshape(*lead, rows, columns)


def kernel(chunks, *refs):
    g_refs, w_refs, m_refs, v_refs = (refs[i : i + 3] for i in (0, 3, 6, 9))
    out_refs, mo_refs, vo_refs = (refs[i : i + 3] for i in (12, 15, 18))
    half_ref, line_ref = refs[21:23]
    own, early, late, s1, s2, recv, sent, near = refs[23:]

    me = lax.axis_index("dp")
    core, chip = me % CORES, me // CORES
    x, y = chip // RING, chip % RING
    mate = 1 - core

    def place(ra, rb):
        return (x + ra * mate + rb * core) % RING * RING + (y + rb * mate + ra * core) % RING

    chips = [[place(ra, rb) for rb in range(RING)] for ra in range(RING)]
    right, left = chips[1][0] * CORES + core, chips[RING - 1][0] * CORES + core
    up, down = chips[0][1] * CORES + core, chips[0][RING - 1] * CORES + core
    partner = chip * CORES + mate

    barrier = pltpu.get_barrier_semaphore()
    peers = (right, left, up, down, partner)
    for peer in peers:
        pl.semaphore_signal(barrier, inc=1, device_id={"dp": peer}, device_id_type=pl.DeviceIdType.MESH)
    pl.semaphore_wait(barrier, len(peers))

    def copy_to(device, src, dst, send_sem, recv_sem):
        pltpu.make_async_remote_copy(
            src_ref=src, dst_ref=dst, send_sem=send_sem, recv_sem=recv_sem, device_id={"dp": device}, device_id_type=pl.DeviceIdType.MESH
        ).start()

    def wait(ref, sem):
        pltpu.make_async_copy(ref, ref, sem).wait()

    kinds = (
        "half", "relay_l", "relay_r", "fl_direct", "fl_relay", "fr_direct", "fr_relay", "relay_d",
        "relay_u", "fd_direct", "fd_relay", "fu_direct", "fu_relay", "g2_d", "g2_u", "g2_far_d",
        "g2_far_u", "g1_l0", "g1_l1", "g1_l2", "g1_l3", "g1_r0", "g1_r1", "g1_r2",
        "g1_r3", "far_0", "far_3", "far_1l", "far_1r", "far_2l", "far_2r", "core",
    )

    def rsem(k, kind):
        return recv.at[k, kinds.index(kind)]

    def total(dst, at, sources, tiles, unroll):
        @pl.loop(0, tiles // unroll)
        def _(i):
            parts = [ref[pl.ds(start + i * unroll, unroll)].astype(F32) for ref, start in sources]
            dst[pl.ds(at + i * unroll, unroll)] = functools.reduce(jnp.add, parts).astype(BF16)

    class Chunk:
        pass

    cs = []
    base = 0
    for k, (weight, layer, t0, nt) in enumerate(chunks):
        c = Chunk()
        c.k, c.weight, c.layer, c.t0, c.nt, c.h, c.base = k, weight, layer, t0, nt, nt // 2, base
        c.own, c.s1, c.s2 = own.at[k % SLOTS], s1.at[k % SLOTS], s2.at[k]
        c.early, c.late = early.at[k % EARLY_SLOTS], late.at[k % SLOTS]
        c.landing = line_ref.at[pl.ds(base // (RING * RING) * 12, 12 * nt)]
        base += RING * RING * nt
        cs.append(c)

    def out_at(c, where, which, t=0, n=None):
        return out_refs[c.weight].at[c.layer, where, which, pl.ds(c.t0 + t, c.nt if n is None else n)]

    def spread(c, where, device, kind, t=0, n=None):
        piece = out_at(c, where, core, t, n)
        copy_to(device, piece, piece, sent.at[c.k, 1], rsem(c.k, kind))

    def send_half(c):
        @pl.loop(0, RING * RING)
        def _(i):
            src = g_refs[c.weight].at[c.layer, place(i % RING, i // RING), mate, pl.ds(c.t0, c.nt)]
            copy_to(partner, src, half_ref.at[pl.ds(c.base + i * c.nt, c.nt)], sent.at[c.k, 1], rsem(c.k, "half"))

    def load_half(c):
        if c.k >= SLOTS:
            old = cs[c.k - SLOTS]
            n = 14 * old.nt
            wait(half_ref.at[pl.ds(0, n)], sent.at[old.k, 0])

        @pl.loop(0, RING * RING)
        def _(i):
            src = g_refs[c.weight].at[c.layer, place(i // RING, i % RING), core, pl.ds(c.t0, c.nt)]
            pltpu.make_async_copy(src, c.own.at[pl.ds(i * c.nt, c.nt)], near.at[c.k, 0]).start()

    def other(c, piece):
        if 6 <= piece < 14:
            return c.early, (piece - 6) * c.nt
        return c.late, (piece if piece < 6 else piece - 8) * c.nt

    def load_other(c):
        nt = c.nt
        wait(half_ref.at[pl.ds(c.base, RING * RING * nt)], rsem(c.k, "half"))
        for i, (dst, to, piece, n) in enumerate(((c.early, 0, 6, 8), (c.late, 0, 0, 6), (c.late, 6, 14, 2))):
            src = half_ref.at[pl.ds(c.base + piece * nt, n * nt)]
            pltpu.make_async_copy(src, dst.at[pl.ds(to * nt, n * nt)], near.at[c.k, (1, 7, 8)[i]]).start()

    def rs1(c):
        nt, n = c.nt, RING * RING * c.nt
        wait(c.own.at[pl.ds(0, n)], near.at[c.k, 0])
        wait(c.early.at[pl.ds(0, 8 * nt)], near.at[c.k, 1])
        for piece, device, at, kind in ((8, right, 0, "relay_l"), (10, left, 2, "relay_r"), (6, right, 6, "fl_direct"), (12, left, 8, "fr_direct")):
            total(c.own, piece * nt, [(c.own, piece * nt), other(c, piece)], 2 * nt, 13)
            copy_to(device, c.own.at[pl.ds(piece * nt, 2 * nt)], c.landing.at[pl.ds(at * nt, 2 * nt)], sent.at[c.k, 0], rsem(c.k, kind))

    def rs1_relay_load(c):
        n = 4 * c.nt
        for at, kind in ((0, "relay_l"), (2, "relay_r")):
            wait(c.landing.at[pl.ds(at * c.nt, 2 * c.nt)], rsem(c.k, kind))
        pltpu.make_async_copy(c.landing.at[pl.ds(0, n)], c.s1.at[pl.ds(0, n)], near.at[c.k, 2]).start()

    def rs1_relay(c):
        nt = c.nt
        wait(c.late.at[pl.ds(0, 6 * nt)], near.at[c.k, 7])
        wait(c.late.at[pl.ds(6 * nt, 2 * nt)], near.at[c.k, 8])
        wait(c.s1.at[pl.ds(0, 4 * nt)], near.at[c.k, 2])
        for piece, device, at, to, kind in ((4, right, 0, 4, "fl_relay"), (14, left, 2, 10, "fr_relay")):
            total(c.s1, at * nt, [(c.own, piece * nt), other(c, piece), (c.s1, at * nt)], 2 * nt, 13)
            copy_to(device, c.s1.at[pl.ds(at * nt, 2 * nt)], c.landing.at[pl.ds(to * nt, 2 * nt)], sent.at[c.k, 0], rsem(c.k, kind))

    def line(c, rb, t):
        nt = c.nt
        return [(c.own, rb * nt + t), (c.late, rb * nt + t), (c.s1, (4 + rb) * nt + t), (c.s1, (8 + rb) * nt + t)]

    def rs2_load(c):
        nt = c.nt
        for at, kind in ((4, "fl_relay"), (6, "fl_direct"), (8, "fr_direct"), (10, "fr_relay")):
            wait(c.landing.at[pl.ds(at * nt, 2 * nt)], rsem(c.k, kind))
        pltpu.make_async_copy(c.landing.at[pl.ds(4 * nt, 8 * nt)], c.s1.at[pl.ds(4 * nt, 8 * nt)], near.at[c.k, 6]).start()

    def rs2(c):
        nt, h = c.nt, c.h
        wait(c.s1.at[pl.ds(4 * nt, 8 * nt)], near.at[c.k, 6])
        for rb, t, n, device, to, kind in (
            (2, 0, h, up, 0, "relay_d"),
            (2, h, nt - h, down, h, "relay_u"),
            (1, h, nt - h, up, nt + h, "fd_direct"),
            (3, 0, h, down, 2 * nt, "fu_direct"),
        ):
            total(c.own, rb * nt + t, line(c, rb, t), n, 13)
            copy_to(device, c.own.at[pl.ds(rb * nt + t, n)], c.s2.at[pl.ds(to, n)], sent.at[c.k, 0], rsem(c.k, kind))

    def rs2_relay(c):
        nt, h = c.nt, c.h
        for rb, t, n, device, to, kind, kind_to in ((1, 0, h, up, nt, "relay_d", "fd_relay"), (3, h, nt - h, down, 2 * nt + h, "relay_u", "fu_relay")):
            here = c.s2.at[pl.ds(t, n)]
            wait(here, rsem(c.k, kind))
            total(c.s2, t, [*line(c, rb, t), (c.s2, t)], n, 13)
            copy_to(device, here, c.s2.at[pl.ds(to, n)], sent.at[c.k, 1], rsem(c.k, kind_to))

    loaded = set()

    def update(c):
        nt, h = c.nt, c.h
        if c.weight not in loaded:
            loaded.add(c.weight)
            for i, (store, src) in enumerate(state(c.weight)):
                wait(store, near.at[c.weight, 3 + i])
        for at, n, kind in ((nt, h, "fd_relay"), (nt + h, nt - h, "fd_direct"), (2 * nt, h, "fu_direct"), (2 * nt + h, nt - h, "fu_relay")):
            wait(c.s2.at[pl.ds(at, n)], rsem(c.k, kind))
        w_store = out_refs[c.weight].at[c.layer, chip, core]
        m_store, v_store = mo_refs[c.weight].at[c.layer], vo_refs[c.weight].at[c.layer]
        sources = [*line(c, 0, 0), (c.s2, nt), (c.s2, 2 * nt)]
        unroll = 4

        @pl.loop(0, nt // unroll)
        def _(i):
            g = functools.reduce(jnp.add, [ref[pl.ds(start + i * unroll, unroll)].astype(F32) for ref, start in sources])
            g = g.astype(BF16).astype(F32)
            here = pl.ds(c.t0 + i * unroll, unroll)
            w = w_store[here].astype(F32)
            m = 0.9 * m_store[here] + 0.1 * g
            v = 0.95 * v_store[here] + 0.05 * g * g
            step = m * lax.rsqrt(v + 1e-8) + 0.1 * w
            w_store[here] = (w - 0.02 * step).astype(BF16)
            m_store[here] = m
            v_store[here] = v

        spread(c, chip, up, "g2_d")
        spread(c, chip, down, "g2_u")

    def ag1_own(c):
        spread(c, chip, right, "g1_l0")
        spread(c, chip, left, "g1_r0")
        spread(c, chip, partner, "core")

    def arrived(c, where, kind, t=0, n=None):
        wait(out_at(c, where, core, t, n), rsem(c.k, kind))

    def ag2_relay(c):
        arrived(c, chips[0][3], "g2_d")
        spread(c, chips[0][3], up, "g2_far_d", 0, c.h)
        arrived(c, chips[0][1], "g2_u")
        spread(c, chips[0][1], down, "g2_far_u", c.h, c.nt - c.h)

    def ag1_near(c):
        for rb in (3, 1):
            spread(c, chips[0][rb], right, f"g1_l{rb}")
            spread(c, chips[0][rb], left, f"g1_r{rb}")
            spread(c, chips[0][rb], partner, "core")

    def ag1_far(c):
        arrived(c, chips[0][2], "g2_far_d", 0, c.h)
        arrived(c, chips[0][2], "g2_far_u", c.h, c.nt - c.h)
        spread(c, chips[0][2], right, "g1_l2")
        spread(c, chips[0][2], left, "g1_r2")
        spread(c, chips[0][2], partner, "core")

    def relay(c, rb):
        for ra, kind in ((3, f"g1_l{rb}"), (1, f"g1_r{rb}")):
            arrived(c, chips[ra][rb], kind)
        if rb == 0:
            spread(c, chips[3][0], right, "far_0")
        elif rb == 3:
            spread(c, chips[1][3], left, "far_3")
        else:
            spread(c, chips[3][rb], right, f"far_{rb}l", 0, c.h)
            spread(c, chips[1][rb], left, f"far_{rb}r", c.h, c.nt - c.h)
        for ra in (3, 1):
            spread(c, chips[ra][rb], partner, "core")

    def ag1_relay(c):
        for rb in (0, 3, 1):
            relay(c, rb)

    def ag1_relay_far(c):
        relay(c, 2)

    def last(c):
        arrived(c, chips[2][0], "far_0")
        arrived(c, chips[2][3], "far_3")
        for rb in (1, 2):
            arrived(c, chips[2][rb], f"far_{rb}l", 0, c.h)
            arrived(c, chips[2][rb], f"far_{rb}r", c.h, c.nt - c.h)
        for rb in range(RING):
            spread(c, chips[2][rb], partner, "core")

    def state(weight):
        mine = w_refs[weight].at[:, chip, core]
        return ((out_refs[weight].at[:, chip, core], mine), (mo_refs[weight], m_refs[weight]), (vo_refs[weight], v_refs[weight]))

    tasks = dict(
        send_half=send_half, load_half=load_half, load_other=load_other, rs1=rs1,
        rs1_relay_load=rs1_relay_load, rs1_relay=rs1_relay, rs2_load=rs2_load, rs2=rs2, rs2_relay=rs2_relay,
        update=update, ag1_own=ag1_own, ag2_relay=ag2_relay, ag1_near=ag1_near, ag1_far=ag1_far, ag1_relay=ag1_relay,
        ag1_relay_far=ag1_relay_far, last=last,
    )
    rank = {name: i for i, name in enumerate(tasks)}
    order = sorted(((TURN[name][0] + TURN[name][1] * c.k, rank[name], name, c) for name in tasks for c in cs), key=lambda one: one[:2])
    turn = {(name, c.k): i for i, (_, _, name, c) in enumerate(order)}
    for k in range(len(cs)):
        assert turn["load_half", k] < turn["load_other", k]
        assert k < SLOTS or turn["update", k - SLOTS] < turn["load_half", k]
        assert k < EARLY_SLOTS or turn["rs1", k - EARLY_SLOTS] < turn["load_other", k]
    state_at = 3
    for i, (_, _, name, c) in enumerate(order):
        if i == state_at:
            for weight in range(3):
                for j, (store, src) in enumerate(state(weight)):
                    pltpu.make_async_copy(src, store, near.at[weight, 3 + j]).start()
        tasks[name](c)

    for c in cs:
        here = pl.ds(c.t0, c.nt)
        wait(out_refs[c.weight].at[c.layer, :, mate, here], rsem(c.k, "core"))
        wait(half_ref.at[pl.ds(0, 48 * c.nt)], sent.at[c.k, 1])
        if c.k >= len(cs) - SLOTS:
            wait(half_ref.at[pl.ds(0, 14 * c.nt)], sent.at[c.k, 0])


def put(*refs):
    n = len(refs) // 2
    srcs, dsts, sem = refs[:n], refs[n : 2 * n], refs[2 * n]
    copies = []
    for src, dst in zip(srcs, dsts, strict=True):
        for layer in range(src.shape[0]):
            step = src.shape[1] // 4
            for part in range(4):
                here = pl.ds(part * step, step)
                copies.append(pltpu.make_async_copy(src.at[layer, here], dst.at[layer, here], sem.at[len(copies)]))
    for copy in copies:
        copy.start()
    for copy in copies:
        copy.wait()


def solution(mesh):
    group = mesh.shape["dp"]
    assert group == CORES * RING * RING and math.isqrt(group // CORES) == RING

    def step(*arrays):
        terms, weights, m, v = (arrays[i : i + 3] for i in (0, 3, 6, 9))
        layers = m[0].shape[0]
        shapes = [one.shape for one in m]
        blocks = [as_tiles(t[0], s[1]) for t, s in zip(terms, shapes, strict=True)]
        blocks += [as_tiles(w, s[1]) for w, s in zip(weights, shapes, strict=True)]
        tiles = blocks[0].shape[2]
        blocks = [b.reshape(layers, RING * RING, CORES, tiles, 8, 128) for b in blocks]
        moments = [as_tiles(one, one.shape[1]).reshape(layers, tiles, 8, 128) for one in (*m, *v)]
        nt = tiles // PER_MATRIX
        chunks = [(weight, layer, part * nt, nt) for weight in range(3) for layer in range(layers) for part in range(PER_MATRIX)]
        count = len(chunks)
        whole = pltpu.VMEM(blocks[0].shape, BF16)
        moment = pltpu.VMEM(moments[0].shape, F32)
        hbm, vmem = pl.BlockSpec(memory_space=pltpu.HBM), pl.BlockSpec(memory_space=pltpu.VMEM)
        pieces = RING * RING
        out = pl.pallas_call(
            functools.partial(kernel, chunks),
            out_shape=[whole] * 3
            + [moment] * 6
            + [jax.ShapeDtypeStruct((count * pieces * nt, 8, 128), BF16), jax.ShapeDtypeStruct((count * 12 * nt, 8, 128), BF16)],
            in_specs=[hbm] * 12,
            out_specs=[vmem] * 9 + [hbm] * 2,
            scratch_shapes=[
                pltpu.VMEM((SLOTS, pieces * nt, 8, 128), BF16),
                pltpu.VMEM((EARLY_SLOTS, 8 * nt, 8, 128), BF16),
                pltpu.VMEM((SLOTS, 8 * nt, 8, 128), BF16),
                pltpu.VMEM((SLOTS, 12 * nt, 8, 128), BF16),
                pltpu.VMEM((count, 3 * nt, 8, 128), BF16),
                pltpu.SemaphoreType.DMA((count, 32)),
                pltpu.SemaphoreType.DMA((count, 2)),
                pltpu.SemaphoreType.DMA((count, 9)),
            ],
            compiler_params=pltpu.CompilerParams(collective_id=0, has_side_effects=True, vmem_limit_bytes=VMEM_LIMIT),
        )(*blocks, *moments)[:9]
        out = [pltpu.with_memory_space_constraint(o, pltpu.VMEM) for o in out]
        out = pl.pallas_call(
            put,
            out_shape=[jax.ShapeDtypeStruct(o.shape, o.dtype) for o in out],
            in_specs=[vmem] * 9,
            out_specs=[hbm] * 9,
            scratch_shapes=[pltpu.SemaphoreType.DMA((4 * layers * 9,))],
            compiler_params=pltpu.CompilerParams(vmem_limit_bytes=VMEM_LIMIT),
        )(*out)
        new = [from_tiles(o.reshape(layers, group, tiles, 8, 128), group * s[1], s[2]) for o, s in zip(out[:3], shapes, strict=True)]
        moved = [from_tiles(o.reshape(layers, 1, tiles, 8, 128), s[1], s[2]) for o, s in zip(out[3:9], shapes * 2, strict=True)]
        return (*new, *moved)

    all_of, cut = P(None, None, None), P(None, "dp", None)
    return jax.shard_map(
        step,
        mesh=mesh,
        in_specs=(P(("rep", "dp"), None, None, None),) * 3 + (all_of,) * 3 + (cut,) * 6,
        out_specs=(P("rep", None, None),) * 3 + (P("rep", "dp", None),) * 6,
        check_vma=False,
    )
```

time: 541 us -> 246 us (0.45)
  waiting for transfers between devices: 458 us -> 0 us
  Pallas kernels: 0 us -> 244 us
  local copies, waits for them, and re-layouts: 59.4 us -> 0 us
  between operations: 14.2 us -> 0.82 us
  other arithmetic: 8.47 us -> 0 us
    pallas_call x0 -> x2, Pallas kernels: none -> 244 us  [the longest x1 229 us: step(): pl.pallas_call(functools.partial(kernel, chunks), out_shape=[whole] * 3 +...]
    all_gather x3 -> x0, waiting for transfers between devices: 184 us -> none  [step(): whole = [lax.all_gather(one[0], 'dp', axis=1, tiled=True) for one in new]]
    reduce_scatter x2 -> x0, waiting for transfers between devices: 173 us -> none  [step(): lax.psum_scatter(t[0], 'dp', scatter_dimension=1, tiled=True)]
    unnamed x7 -> x0, waiting for transfers between devices: 102 us -> none
    unnamed x24 -> x0, local copies, waits for them, and re-layouts: 59.4 us -> none
    convert_element_type x3 -> x0, other arithmetic: 8.47 us -> none  [adamw(): return ((w - 0.02 * step).astype(jnp.bfloat16), m, v)]
  transfers between devices with their start and end apart: 6 -> 0, of which waited for: 6 -> 0; matrix products, arithmetic and copies ran while one was open for 8% -> 0% of each run, Pallas kernels for 0% -> 0%
where the time goes in v1:
time: 246 us; the launch traced here: 245 us
  Pallas kernels  244 us (99%)
    pallas_call x1, Pallas kernels, step(): pl.pallas_call(functools.partial(kernel, chunks), out_shape=[whole] * 3 +...  229 us
    pallas_call x1, Pallas kernels, step(): pl.pallas_call(put, out_shape=[jax.ShapeDtypeStruct(o.shape, o.dtype) for...  15.2 us

profile of v1, /device:TPU:97, one launch (start us, length us, event | category | flops | bytes accessed | tf_op | source)
XLA Modules:
  0.0 244.9 jit_solution(1867285385795421772)
XLA Ops:
  0.6 228.8 %shard_map.187 = (bf16[2,16,2,104,8,128]{5,4,3,2,1,0:T(8,128)(2,1)S(1)}, bf16[2,16,2,104,8,128]{5,4,3,2,1,0:T(8,128)(2,1)S(1)}, bf16[2,16,2,104,8,128]{5,4,3,2,1...) custom-call(bf16[2,16,2,104,8,128]{5,4,3,2,1,0:T(8,128)(2,1)} %bitca, ...), custom_call_target="tpu_custom_call" | custom-call | tf_op jit(solution)/shard_map/pallas_call | solution.py:344
  229.5 15.2 %shard_map.188 = (bf16[2,16,2,104,8,128]{5,4,3,2,1,0:T(8,128)(2,1)}, bf16[2,16,2,104,8,128]{5,4,3,2,1,0:T(8,128)(2,1)}, bf16[2,16,2,104,8,128]{5,4,3,2,1,0:T(8,1...) custom-call(bf16[2,16,2,104,8,128]{5,4,3,2,1,0:T(8,128)(2,1)S(1)} %g, ...), custom_call_target="tpu_custom_call" | custom-call | tf_op jit(solution)/shard_map/pallas_call | solution.py:364

commit v2 on v1

--- a/solution.py
+++ b/solution.py
@@ -67,7 +67,7 @@
         pltpu.make_async_copy(ref, ref, sem).wait()
 
     kinds = (
-        "half", "relay_l", "relay_r", "fl_direct", "fl_relay", "fr_direct", "fr_relay", "relay_d",
+        "half_0", "half_1", "half_2", "half_3", "half_4", "relay_l", "relay_r", "fl_direct", "fl_relay", "fr_direct", "fr_relay", "relay_d",
         "relay_u", "fd_direct", "fd_relay", "fu_direct", "fu_relay", "g2_d", "g2_u", "g2_far_d",
         "g2_far_u", "g1_l0", "g1_l1", "g1_l2", "g1_l3", "g1_r0", "g1_r1", "g1_r2",
         "g1_r3", "far_0", "far_3", "far_1l", "far_1r", "far_2l", "far_2r", "core",
@@ -92,7 +92,8 @@
         c.k, c.weight, c.layer, c.t0, c.nt, c.h, c.base = k, weight, layer, t0, nt, nt // 2, base
         c.own, c.s1, c.s2 = own.at[k % SLOTS], s1.at[k % SLOTS], s2.at[k]
         c.early, c.late = early.at[k % EARLY_SLOTS], late.at[k % SLOTS]
-        c.landing = line_ref.at[pl.ds(base // (RING * RING) * 12, 12 * nt)]
+        c.half_direct, c.line_direct = k < EARLY_SLOTS, k < SLOTS
+        c.landing = c.s1 if c.line_direct else line_ref.at[pl.ds(base // (RING * RING) * 12, 12 * nt)]
         base += RING * RING * nt
         cs.append(c)
 
@@ -103,11 +104,24 @@
         piece = out_at(c, where, core, t, n)
         copy_to(device, piece, piece, sent.at[c.k, 1], rsem(c.k, kind))
 
+    runs = ((8, 12), (6, 8), (12, 14), (0, 6), (14, 16))
+
+    def other(c, piece):
+        if 6 <= piece < 14:
+            return c.early, (piece - 6) * c.nt
+        return c.late, (piece if piece < 6 else piece - 8) * c.nt
+
+    def half(c, piece):
+        return other(c, piece) if c.half_direct else (half_ref, c.base + piece * c.nt)
+
     def send_half(c):
-        @pl.loop(0, RING * RING)
-        def _(i):
-            src = g_refs[c.weight].at[c.layer, place(i % RING, i // RING), mate, pl.ds(c.t0, c.nt)]
-            copy_to(partner, src, half_ref.at[pl.ds(c.base + i * c.nt, c.nt)], sent.at[c.k, 1], rsem(c.k, "half"))
+        for run, (first, end) in enumerate(runs):
+            dst, at = half(c, first)
+
+            @pl.loop(first, end)
+            def _(i):
+                src = g_refs[c.weight].at[c.layer, place(i % RING, i // RING), mate, pl.ds(c.t0, c.nt)]
+                copy_to(partner, src, dst.at[pl.ds(at + (i - first) * c.nt, c.nt)], sent.at[c.k, 1], rsem(c.k, f"half_{run}"))
 
     def load_half(c):
         if c.k >= SLOTS:
@@ -115,59 +129,90 @@
             n = 14 * old.nt
             wait(half_ref.at[pl.ds(0, n)], sent.at[old.k, 0])
 
-        @pl.loop(0, RING * RING)
-        def _(i):
-            src = g_refs[c.weight].at[c.layer, place(i // RING, i % RING), core, pl.ds(c.t0, c.nt)]
-            pltpu.make_async_copy(src, c.own.at[pl.ds(i * c.nt, c.nt)], near.at[c.k, 0]).start()
-
-    def other(c, piece):
-        if 6 <= piece < 14:
-            return c.early, (piece - 6) * c.nt
-        return c.late, (piece if piece < 6 else piece - 8) * c.nt
+        for run, (first, end) in enumerate(runs):
+
+            @pl.loop(first, end)
+            def _(i):
+                src = g_refs[c.weight].at[c.layer, place(i // RING, i % RING), core, pl.ds(c.t0, c.nt)]
+                pltpu.make_async_copy(src, c.own.at[pl.ds(i * c.nt, c.nt)], near.at[c.k, 9 + run]).start()
+
+    def half_arrived(c, run):
+        first, end = runs[run]
+        dst, at = half(c, first)
+        wait(dst.at[pl.ds(at, (end - first) * c.nt)], rsem(c.k, f"half_{run}"))
+
+    def own_arrived(c, run):
+        first, end = runs[run]
+        wait(c.own.at[pl.ds(first * c.nt, (end - first) * c.nt)], near.at[c.k, 9 + run])
 
     def load_other(c):
         nt = c.nt
-        wait(half_ref.at[pl.ds(c.base, RING * RING * nt)], rsem(c.k, "half"))
+        if c.half_direct:
+            return
+        for run in range(len(runs)):
+            half_arrived(c, run)
         for i, (dst, to, piece, n) in enumerate(((c.early, 0, 6, 8), (c.late, 0, 0, 6), (c.late, 6, 14, 2))):
             src = half_ref.at[pl.ds(c.base + piece * nt, n * nt)]
             pltpu.make_async_copy(src, dst.at[pl.ds(to * nt, n * nt)], near.at[c.k, (1, 7, 8)[i]]).start()
 
     def rs1(c):
-        nt, n = c.nt, RING * RING * c.nt
-        wait(c.own.at[pl.ds(0, n)], near.at[c.k, 0])
-        wait(c.early.at[pl.ds(0, 8 * nt)], near.at[c.k, 1])
-        for piece, device, at, kind in ((8, right, 0, "relay_l"), (10, left, 2, "relay_r"), (6, right, 6, "fl_direct"), (12, left, 8, "fr_direct")):
-            total(c.own, piece * nt, [(c.own, piece * nt), other(c, piece)], 2 * nt, 13)
-            copy_to(device, c.own.at[pl.ds(piece * nt, 2 * nt)], c.landing.at[pl.ds(at * nt, 2 * nt)], sent.at[c.k, 0], rsem(c.k, kind))
+        nt = c.nt
+        if not c.half_direct:
+            wait(c.early.at[pl.ds(0, 8 * nt)], near.at[c.k, 1])
+        for run, sends in enumerate((((8, right, 0, "relay_l"), (10, left, 2, "relay_r")), ((6, right, 6, "fl_direct"),), ((12, left, 8, "fr_direct"),))):
+            own_arrived(c, run)
+            if c.half_direct:
+                half_arrived(c, run)
+            for piece, device, at, kind in sends:
+                total(c.own, piece * nt, [(c.own, piece * nt), other(c, piece)], 2 * nt, 13)
+                copy_to(device, c.own.at[pl.ds(piece * nt, 2 * nt)], c.landing.at[pl.ds(at * nt, 2 * nt)], sent.at[c.k, 0], rsem(c.k, kind))
 
     def rs1_relay_load(c):
         n = 4 * c.nt
+        if c.line_direct:
+            return
         for at, kind in ((0, "relay_l"), (2, "relay_r")):
             wait(c.landing.at[pl.ds(at * c.nt, 2 * c.nt)], rsem(c.k, kind))
         pltpu.make_async_copy(c.landing.at[pl.ds(0, n)], c.s1.at[pl.ds(0, n)], near.at[c.k, 2]).start()
 
     def rs1_relay(c):
         nt = c.nt
-        wait(c.late.at[pl.ds(0, 6 * nt)], near.at[c.k, 7])
-        wait(c.late.at[pl.ds(6 * nt, 2 * nt)], near.at[c.k, 8])
-        wait(c.s1.at[pl.ds(0, 4 * nt)], near.at[c.k, 2])
-        for piece, device, at, to, kind in ((4, right, 0, 4, "fl_relay"), (14, left, 2, 10, "fr_relay")):
+        for run in (3, 4):
+            own_arrived(c, run)
+            if c.half_direct:
+                half_arrived(c, run)
+        if not c.half_direct:
+            wait(c.late.at[pl.ds(0, 6 * nt)], near.at[c.k, 7])
+            wait(c.late.at[pl.ds(6 * nt, 2 * nt)], near.at[c.k, 8])
+        if not c.line_direct:
+            wait(c.s1.at[pl.ds(0, 4 * nt)], near.at[c.k, 2])
+        for piece, device, at, to, kind, kind_to in ((4, right, 0, 4, "relay_l", "fl_relay"), (14, left, 2, 10, "relay_r", "fr_relay")):
+            if c.line_direct:
+                wait(c.s1.at[pl.ds(at * nt, 2 * nt)], rsem(c.k, kind))
             total(c.s1, at * nt, [(c.own, piece * nt), other(c, piece), (c.s1, at * nt)], 2 * nt, 13)
-            copy_to(device, c.s1.at[pl.ds(at * nt, 2 * nt)], c.landing.at[pl.ds(to * nt, 2 * nt)], sent.at[c.k, 0], rsem(c.k, kind))
+            copy_to(device, c.s1.at[pl.ds(at * nt, 2 * nt)], c.landing.at[pl.ds(to * nt, 2 * nt)], sent.at[c.k, 0], rsem(c.k, kind_to))
 
     def line(c, rb, t):
         nt = c.nt
         return [(c.own, rb * nt + t), (c.late, rb * nt + t), (c.s1, (4 + rb) * nt + t), (c.s1, (8 + rb) * nt + t)]
 
+    def line_arrived(c):
+        for at, kind in ((4, "fl_relay"), (6, "fl_direct"), (8, "fr_direct"), (10, "fr_relay")):
+            wait(c.landing.at[pl.ds(at * c.nt, 2 * c.nt)], rsem(c.k, kind))
+
     def rs2_load(c):
         nt = c.nt
-        for at, kind in ((4, "fl_relay"), (6, "fl_direct"), (8, "fr_direct"), (10, "fr_relay")):
-            wait(c.landing.at[pl.ds(at * nt, 2 * nt)], rsem(c.k, kind))
+        if c.line_direct:
+            return
+        line_arrived(c)
         pltpu.make_async_copy(c.landing.at[pl.ds(4 * nt, 8 * nt)], c.s1.at[pl.ds(4 * nt, 8 * nt)], near.at[c.k, 6]).start()
 
     def rs2(c):
         nt, h = c.nt, c.h
-        wait(c.s1.at[pl.ds(4 * nt, 8 * nt)], near.at[c.k, 6])
+        if c.line_direct:
+            line_arrived(c)
+        else:
+            wait(c.s1.at[pl.ds(4 * nt, 8 * nt)], near.at[c.k, 6])
         for rb, t, n, device, to, kind in (
             (2, 0, h, up, 0, "relay_d"),
             (2, h, nt - h, down, h, "relay_u"),
@@ -289,13 +334,12 @@
         assert turn["load_half", k] < turn["load_other", k]
         assert k < SLOTS or turn["update", k - SLOTS] < turn["load_half", k]
         assert k < EARLY_SLOTS or turn["rs1", k - EARLY_SLOTS] < turn["load_other", k]
-    state_at = 3
-    for i, (_, _, name, c) in enumerate(order):
-        if i == state_at:
+    for _, _, name, c in order:
+        tasks[name](c)
+        if name == "rs1" and c.k == 0:
             for weight in range(3):
                 for j, (store, src) in enumerate(state(weight)):
                     pltpu.make_async_copy(src, store, near.at[weight, 3 + j]).start()
-        tasks[name](c)
 
     for c in cs:
         here = pl.ds(c.t0, c.nt)
@@ -354,9 +398,9 @@
                 pltpu.VMEM((SLOTS, 8 * nt, 8, 128), BF16),
                 pltpu.VMEM((SLOTS, 12 * nt, 8, 128), BF16),
                 pltpu.VMEM((count, 3 * nt, 8, 128), BF16),
-                pltpu.SemaphoreType.DMA((count, 32)),
+                pltpu.SemaphoreType.DMA((count, 36)),
                 pltpu.SemaphoreType.DMA((count, 2)),
-                pltpu.SemaphoreType.DMA((count, 9)),
+                pltpu.SemaphoreType.DMA((count, 14)),
             ],
             compiler_params=pltpu.CompilerParams(collective_id=0, has_side_effects=True, vmem_limit_bytes=VMEM_LIMIT),
         )(*blocks, *moments)[:9]

time: 246 us -> 241 us (0.980)
  Pallas kernels: 244 us -> 240 us
    pallas_call x1, Pallas kernels: 229 us -> 225 us  [step(): pl.pallas_call(functools.partial(kernel, chunks), out_shape=[whole] * 3 +...]
where the time goes in v2:
time: 241 us
  Pallas kernels  240 us (100%)
    pallas_call x1, Pallas kernels, step(): pl.pallas_call(functools.partial(kernel, chunks), out_shape=[whole] * 3 +...  225 us
    pallas_call x1, Pallas kernels, step(): pl.pallas_call(put, out_shape=[jax.ShapeDtypeStruct(o.shape, o.dtype) for...  15.2 us

profile of v2, /device:TPU:97, one launch (start us, length us, event | category | flops | bytes accessed | tf_op | source)
XLA Modules:
  0.0 240.8 jit_solution(12583822676291656598)
XLA Ops:
  0.6 224.7 %shard_map.187 = (bf16[2,16,2,104,8,128]{5,4,3,2,1,0:T(8,128)(2,1)S(1)}, bf16[2,16,2,104,8,128]{5,4,3,2,1,0:T(8,128)(2,1)S(1)}, bf16[2,16,2,104,8,128]{5,4,3,2,1...) custom-call(bf16[2,16,2,104,8,128]{5,4,3,2,1,0:T(8,128)(2,1)} %bitca, ...), custom_call_target="tpu_custom_call" | custom-call | tf_op jit(solution)/shard_map/pallas_call | solution.py:388
  225.4 15.2 %shard_map.188 = (bf16[2,16,2,104,8,128]{5,4,3,2,1,0:T(8,128)(2,1)}, bf16[2,16,2,104,8,128]{5,4,3,2,1,0:T(8,128)(2,1)}, bf16[2,16,2,104,8,128]{5,4,3,2,1,0:T(8,1...) custom-call(bf16[2,16,2,104,8,128]{5,4,3,2,1,0:T(8,128)(2,1)S(1)} %g, ...), custom_call_target="tpu_custom_call" | custom-call | tf_op jit(solution)/shard_map/pallas_call | solution.py:408

commit v3 on v2

--- a/solution.py
+++ b/solution.py
@@ -16,7 +16,7 @@
 EARLY_SLOTS = 2
 SLOTS = 3
 
-TURN = {'send_half': (-17.7, 10.6), 'load_half': (-8.4, 10.6), 'load_other': (-8.0, 10.6), 'rs1': (-3.6, 10.6), 'rs1_relay_load': (3.5, 10.6), 'rs1_relay': (5.0, 10.6), 'rs2_load': (12.4, 10.6), 'rs2': (13.3, 10.6), 'rs2_relay': (17.1, 10.6), 'update': (21.6, 10.6), 'ag1_own': (24.0, 12.24), 'ag2_relay': (24.8, 12.24), 'ag1_near': (25.3, 12.24), 'ag1_far': (31.0, 12.24), 'ag1_relay': (44.8, 12.24), 'ag1_relay_far': (48.3, 12.24), 'last': (66.1, 12.24)}
+TURN = {'send_half': (-12.6, 9.9), 'load_half': (-7.3, 9.9), 'load_other': (-7.1, 9.9), 'rs1': (-3.4, 9.9), 'rs1_relay_load': (4.3, 9.9), 'rs1_relay': (4.9, 9.9), 'rs2_load': (10.7, 9.9), 'rs2': (11.8, 9.9), 'rs2_relay': (18.6, 9.9), 'update': (21.8, 9.9), 'ag1_own': (24.9, 11.13), 'ag2_relay': (26.6, 11.13), 'ag1_near': (27.4, 11.13), 'ag1_far': (34.6, 11.13), 'ag1_relay': (49.9, 11.13), 'ag1_relay_far': (55.7, 11.13), 'last': (74.6, 11.13)}
 
 
 def as_tiles(a, rows):
@@ -53,7 +53,8 @@
     partner = chip * CORES + mate
 
     barrier = pltpu.get_barrier_semaphore()
-    peers = (right, left, up, down, partner)
+    right_mate, left_mate = chips[1][0] * CORES + mate, chips[RING - 1][0] * CORES + mate
+    peers = (right, left, up, down, partner, right_mate, left_mate)
     for peer in peers:
         pl.semaphore_signal(barrier, inc=1, device_id={"dp": peer}, device_id_type=pl.DeviceIdType.MESH)
     pl.semaphore_wait(barrier, len(peers))
@@ -67,7 +68,7 @@
         pltpu.make_async_copy(ref, ref, sem).wait()
 
     kinds = (
-        "half_0", "half_1", "half_2", "half_3", "half_4", "relay_l", "relay_r", "fl_direct", "fl_relay", "fr_direct", "fr_relay", "relay_d",
+        "half_0", "half_1", "half_2", "half_3", "half_4", "half_5", "relay_l", "relay_r", "fl_direct", "fl_relay", "fr_direct", "fr_relay", "relay_d",
         "relay_u", "fd_direct", "fd_relay", "fu_direct", "fu_relay", "g2_d", "g2_u", "g2_far_d",
         "g2_far_u", "g1_l0", "g1_l1", "g1_l2", "g1_l3", "g1_r0", "g1_r1", "g1_r2",
         "g1_r3", "far_0", "far_3", "far_1l", "far_1r", "far_2l", "far_2r", "core",
@@ -104,7 +105,7 @@
         piece = out_at(c, where, core, t, n)
         copy_to(device, piece, piece, sent.at[c.k, 1], rsem(c.k, kind))
 
-    runs = ((8, 12), (6, 8), (12, 14), (0, 6), (14, 16))
+    runs = ((8, 10), (10, 12), (6, 8), (12, 14), (0, 6), (14, 16))
 
     def other(c, piece):
         if 6 <= piece < 14:
@@ -159,13 +160,13 @@
         nt = c.nt
         if not c.half_direct:
             wait(c.early.at[pl.ds(0, 8 * nt)], near.at[c.k, 1])
-        for run, sends in enumerate((((8, right, 0, "relay_l"), (10, left, 2, "relay_r")), ((6, right, 6, "fl_direct"),), ((12, left, 8, "fr_direct"),))):
+        sends = ((8, right, 0, "relay_l"), (10, left, 2, "relay_r"), (6, right, 6, "fl_direct"), (12, left, 8, "fr_direct"))
+        for run, (piece, device, at, kind) in enumerate(sends):
             own_arrived(c, run)
             if c.half_direct:
                 half_arrived(c, run)
-            for piece, device, at, kind in sends:
-                total(c.own, piece * nt, [(c.own, piece * nt), other(c, piece)], 2 * nt, 13)
-                copy_to(device, c.own.at[pl.ds(piece * nt, 2 * nt)], c.landing.at[pl.ds(at * nt, 2 * nt)], sent.at[c.k, 0], rsem(c.k, kind))
+            total(c.own, piece * nt, [(c.own, piece * nt), other(c, piece)], 2 * nt, 13)
+            copy_to(device, c.own.at[pl.ds(piece * nt, 2 * nt)], c.landing.at[pl.ds(at * nt, 2 * nt)], sent.at[c.k, 0], rsem(c.k, kind))
 
     def rs1_relay_load(c):
         n = 4 * c.nt
@@ -177,7 +178,7 @@
 
     def rs1_relay(c):
         nt = c.nt
-        for run in (3, 4):
+        for run in (4, 5):
             own_arrived(c, run)
             if c.half_direct:
                 half_arrived(c, run)
@@ -288,6 +289,9 @@
         spread(c, chips[0][2], left, "g1_r2")
         spread(c, chips[0][2], partner, "core")
 
+    def straight(c, rb):
+        return rb == 2 and c is cs[-1]
+
     def relay(c, rb):
         for ra, kind in ((3, f"g1_l{rb}"), (1, f"g1_r{rb}")):
             arrived(c, chips[ra][rb], kind)
@@ -298,6 +302,9 @@
         else:
             spread(c, chips[3][rb], right, f"far_{rb}l", 0, c.h)
             spread(c, chips[1][rb], left, f"far_{rb}r", c.h, c.nt - c.h)
+            if straight(c, rb):
+                spread(c, chips[3][rb], right_mate, "core", 0, c.h)
+                spread(c, chips[1][rb], left_mate, "core", c.h, c.nt - c.h)
         for ra in (3, 1):
             spread(c, chips[ra][rb], partner, "core")
 
@@ -309,13 +316,14 @@
         relay(c, 2)
 
     def last(c):
-        arrived(c, chips[2][0], "far_0")
-        arrived(c, chips[2][3], "far_3")
-        for rb in (1, 2):
-            arrived(c, chips[2][rb], f"far_{rb}l", 0, c.h)
-            arrived(c, chips[2][rb], f"far_{rb}r", c.h, c.nt - c.h)
-        for rb in range(RING):
-            spread(c, chips[2][rb], partner, "core")
+        for rb in (0, 3, 1, 2):
+            if rb in (0, 3):
+                arrived(c, chips[2][rb], f"far_{rb}")
+            else:
+                arrived(c, chips[2][rb], f"far_{rb}l", 0, c.h)
+                arrived(c, chips[2][rb], f"far_{rb}r", c.h, c.nt - c.h)
+            if not straight(c, rb):
+                spread(c, chips[2][rb], partner, "core")
 
     def state(weight):
         mine = w_refs[weight].at[:, chip, core]
@@ -398,9 +406,9 @@
                 pltpu.VMEM((SLOTS, 8 * nt, 8, 128), BF16),
                 pltpu.VMEM((SLOTS, 12 * nt, 8, 128), BF16),
                 pltpu.VMEM((count, 3 * nt, 8, 128), BF16),
-                pltpu.SemaphoreType.DMA((count, 36)),
+                pltpu.SemaphoreType.DMA((count, 37)),
                 pltpu.SemaphoreType.DMA((count, 2)),
-                pltpu.SemaphoreType.DMA((count, 14)),
+                pltpu.SemaphoreType.DMA((count, 15)),
             ],
             compiler_params=pltpu.CompilerParams(collective_id=0, has_side_effects=True, vmem_limit_bytes=VMEM_LIMIT),
         )(*blocks, *moments)[:9]

time: 241 us -> 240 us (level)
  no operation moved by 1% of the time
where the time goes in v3:
time: 240 us
  Pallas kernels  239 us (100%)
    pallas_call x1, Pallas kernels, step(): pl.pallas_call(functools.partial(kernel, chunks), out_shape=[whole] * 3 +...  224 us
    pallas_call x1, Pallas kernels, step(): pl.pallas_call(put, out_shape=[jax.ShapeDtypeStruct(o.shape, o.dtype) for...  15.2 us

profile of v3, /device:TPU:97, one launch (start us, length us, event | category | flops | bytes accessed | tf_op | source)
XLA Modules:
  0.0 239.6 jit_solution(9868350052220761891)
XLA Ops:
  0.6 223.6 %shard_map.187 = (bf16[2,16,2,104,8,128]{5,4,3,2,1,0:T(8,128)(2,1)S(1)}, bf16[2,16,2,104,8,128]{5,4,3,2,1,0:T(8,128)(2,1)S(1)}, bf16[2,16,2,104,8,128]{5,4,3,2,1...) custom-call(bf16[2,16,2,104,8,128]{5,4,3,2,1,0:T(8,128)(2,1)} %bitca, ...), custom_call_target="tpu_custom_call" | custom-call | tf_op jit(solution)/shard_map/pallas_call | solution.py:396
  224.2 15.2 %shard_map.188 = (bf16[2,16,2,104,8,128]{5,4,3,2,1,0:T(8,128)(2,1)}, bf16[2,16,2,104,8,128]{5,4,3,2,1,0:T(8,128)(2,1)}, bf16[2,16,2,104,8,128]{5,4,3,2,1,0:T(8,1...) custom-call(bf16[2,16,2,104,8,128]{5,4,3,2,1,0:T(8,128)(2,1)S(1)} %g, ...), custom_call_target="tpu_custom_call" | custom-call | tf_op jit(solution)/shard_map/pallas_call | solution.py:416

commit v4 on v3

--- a/solution.py
+++ b/solution.py
@@ -14,6 +14,7 @@
 PER_MATRIX = 2
 VMEM_LIMIT = 17050 << 10
 EARLY_SLOTS = 2
+AHEAD = 2
 SLOTS = 3
 
 TURN = {'send_half': (-12.6, 9.9), 'load_half': (-7.3, 9.9), 'load_other': (-7.1, 9.9), 'rs1': (-3.4, 9.9), 'rs1_relay_load': (4.3, 9.9), 'rs1_relay': (4.9, 9.9), 'rs2_load': (10.7, 9.9), 'rs2': (11.8, 9.9), 'rs2_relay': (18.6, 9.9), 'update': (21.8, 9.9), 'ag1_own': (24.9, 11.13), 'ag2_relay': (26.6, 11.13), 'ag1_near': (27.4, 11.13), 'ag1_far': (34.6, 11.13), 'ag1_relay': (49.9, 11.13), 'ag1_relay_far': (55.7, 11.13), 'last': (74.6, 11.13)}
@@ -57,7 +58,6 @@
     peers = (right, left, up, down, partner, right_mate, left_mate)
     for peer in peers:
         pl.semaphore_signal(barrier, inc=1, device_id={"dp": peer}, device_id_type=pl.DeviceIdType.MESH)
-    pl.semaphore_wait(barrier, len(peers))
 
     def copy_to(device, src, dst, send_sem, recv_sem):
         pltpu.make_async_remote_copy(
@@ -118,13 +118,31 @@
     def send_half(c):
         for run, (first, end) in enumerate(runs):
             dst, at = half(c, first)
+            if c.k == 0 and run < AHEAD:
+                n = (end - first) * c.nt
+                wait(ahead(run, n), near.at[0, 15 + run])
+                copy_to(partner, ahead(run, n), dst.at[pl.ds(at, n)], sent.at[0, 2], rsem(0, f"half_{run}"))
+                continue
 
             @pl.loop(first, end)
             def _(i):
                 src = g_refs[c.weight].at[c.layer, place(i % RING, i // RING), mate, pl.ds(c.t0, c.nt)]
                 copy_to(partner, src, dst.at[pl.ds(at + (i - first) * c.nt, c.nt)], sent.at[c.k, 1], rsem(c.k, f"half_{run}"))
 
+    def ahead(run, n):
+        return own.at[SLOTS - 1, pl.ds(2 * run * cs[0].nt, n)]
+
+    def load_ahead(c):
+        for run, (first, end) in enumerate(runs[:AHEAD]):
+
+            @pl.loop(first, end)
+            def _(i):
+                src = g_refs[c.weight].at[c.layer, place(i % RING, i // RING), mate, pl.ds(c.t0, c.nt)]
+                pltpu.make_async_copy(src, ahead(run, 2 * c.nt).at[pl.ds((i - first) * c.nt, c.nt)], near.at[0, 15 + run]).start()
+
     def load_half(c):
+        if c.k == SLOTS - 1:
+            wait(half_ref.at[pl.ds(0, 2 * AHEAD * cs[0].nt)], sent.at[0, 2])
         if c.k >= SLOTS:
             old = cs[c.k - SLOTS]
             n = 14 * old.nt
@@ -342,8 +360,12 @@
         assert turn["load_half", k] < turn["load_other", k]
         assert k < SLOTS or turn["update", k - SLOTS] < turn["load_half", k]
         assert k < EARLY_SLOTS or turn["rs1", k - EARLY_SLOTS] < turn["load_other", k]
+    load_ahead(cs[0])
+    load_half(cs[0])
+    pl.semaphore_wait(barrier, len(peers))
     for _, _, name, c in order:
-        tasks[name](c)
+        if name != "load_half" or c.k > 0:
+            tasks[name](c)
         if name == "rs1" and c.k == 0:
             for weight in range(3):
                 for j, (store, src) in enumerate(state(weight)):
@@ -352,7 +374,7 @@
     for c in cs:
         here = pl.ds(c.t0, c.nt)
         wait(out_refs[c.weight].at[c.layer, :, mate, here], rsem(c.k, "core"))
-        wait(half_ref.at[pl.ds(0, 48 * c.nt)], sent.at[c.k, 1])
+        wait(half_ref.at[pl.ds(0, (48 if c.k else 48 - 2 * AHEAD) * c.nt)], sent.at[c.k, 1])
         if c.k >= len(cs) - SLOTS:
             wait(half_ref.at[pl.ds(0, 14 * c.nt)], sent.at[c.k, 0])
 
@@ -407,8 +429,8 @@
                 pltpu.VMEM((SLOTS, 12 * nt, 8, 128), BF16),
                 pltpu.VMEM((count, 3 * nt, 8, 128), BF16),
                 pltpu.SemaphoreType.DMA((count, 37)),
-                pltpu.SemaphoreType.DMA((count, 2)),
-                pltpu.SemaphoreType.DMA((count, 15)),
+                pltpu.SemaphoreType.DMA((count, 3)),
+                pltpu.SemaphoreType.DMA((count, 17)),
             ],
             compiler_params=pltpu.CompilerParams(collective_id=0, has_side_effects=True, vmem_limit_bytes=VMEM_LIMIT),
         )(*blocks, *moments)[:9]

time: 240 us -> 240 us (level)
  no operation moved by 1% of the time
where the time goes in v4:
time: 240 us
  Pallas kernels  239 us (100%)
    pallas_call x1, Pallas kernels, step(): pl.pallas_call(functools.partial(kernel, chunks), out_shape=[whole] * 3 +...  224 us
    pallas_call x1, Pallas kernels, step(): pl.pallas_call(put, out_shape=[jax.ShapeDtypeStruct(o.shape, o.dtype) for...  15.2 us

profile of v4, /device:TPU:97, one launch (start us, length us, event | category | flops | bytes accessed | tf_op | source)
XLA Modules:
  0.0 239.6 jit_solution(13218737542442373187)
XLA Ops:
  0.6 223.5 %shard_map.187 = (bf16[2,16,2,104,8,128]{5,4,3,2,1,0:T(8,128)(2,1)S(1)}, bf16[2,16,2,104,8,128]{5,4,3,2,1,0:T(8,128)(2,1)S(1)}, bf16[2,16,2,104,8,128]{5,4,3,2,1...) custom-call(bf16[2,16,2,104,8,128]{5,4,3,2,1,0:T(8,128)(2,1)} %bitca, ...), custom_call_target="tpu_custom_call" | custom-call | tf_op jit(solution)/shard_map/pallas_call | solution.py:418
  224.2 15.2 %shard_map.188 = (bf16[2,16,2,104,8,128]{5,4,3,2,1,0:T(8,128)(2,1)}, bf16[2,16,2,104,8,128]{5,4,3,2,1,0:T(8,128)(2,1)}, bf16[2,16,2,104,8,128]{5,4,3,2,1,0:T(8,1...) custom-call(bf16[2,16,2,104,8,128]{5,4,3,2,1,0:T(8,128)(2,1)S(1)} %g, ...), custom_call_target="tpu_custom_call" | custom-call | tf_op jit(solution)/shard_map/pallas_call | solution.py:438
